TPU v7x, 256 devices: a whole 4x4x8 slice. The times are simulated.
256 devices in a mesh: row: 16 (over x, y_hi, core), col: 16 (over y_lo, z).
Axes of the slice: x: 4, y: 4 (y_hi: 2, y_lo: 2; y = y_hi * 2 + y_lo), z: 8, core: 2. Of those that a mesh axis runs over, the one named last changes fastest.
Arguments:
- points: bfloat16 [32768, 128], P(('row', 'col')), may hold values from -6 to 6
- abar: bfloat16 [32768, 16, 16, 128], P('row', None, 'col'), may hold values from -6 to 6
- inv_scale: float32 [128], replicated, may hold values from 0.05 to 0.2
Outputs:
- point_grad: float32 [32768, 128], P(('row', 'col'))
All inputs are finite; a program needn't handle non-finite values.
Results may differ from a plain program's by a relative error of at most 0.0052.
Values may be sent and summed in bfloat16 or wider, within the bound.
A program may use at most 64 MiB of HBM per device.

v0:
```python
import jax
import jax.numpy as jnp
from jax import lax
from jax.sharding import PartitionSpec as P


def from_everyone(array, axis):
    copies = jnp.broadcast_to(array, (lax.axis_size(axis), *array.shape))
    return lax.all_to_all(copies, axis, split_axis=0, concat_axis=0, tiled=True)


def in_order(parts, dim):
    parts = jnp.moveaxis(parts, 0, dim)
    shape = parts.shape
    return parts.reshape(*shape[:dim], shape[dim] * shape[dim + 1], *shape[dim + 2 :])


def collect(array, axis, dim):
    parts = from_everyone(array, axis)
    return in_order(parts, dim)


def in_blocks(array, dim, peers):
    before, after = (array.shape[:dim], array.shape[dim + 1 :])
    return jnp.moveaxis(array.reshape(*before, peers, -1, *after), dim, 0)


def sent_and_summed(array, axis, dim):
    parts = in_blocks(array, dim, lax.axis_size(axis))
    arrived = lax.all_to_all(parts, axis, split_axis=0, concat_axis=0, tiled=True)
    return arrived.astype(jnp.float32).sum(axis=0)


def kernel_weights(left_scaled, left_sq, right_scaled, right_sq, factors):
    inner = lax.dot_general(
        left_scaled, right_scaled, (((1,), (1,)), ((), ())), preferred_element_type=jnp.float32
    )
    dist = left_sq[:, None] + right_sq[None, :] - 2.0 * inner
    return (factors.astype(jnp.float32) * jnp.exp(-0.5 * dist)).astype(jnp.bfloat16)


def per_device(points, abar, inv_scale):
    scaled = (points.astype(jnp.float32) * inv_scale[None, :]).astype(jnp.bfloat16)
    rows_scaled = collect(scaled, "col", 0)
    cols_scaled = collect(scaled, "row", 0)
    row_count = rows_scaled.shape[0]
    col_count = cols_scaled.shape[0]
    tile = abar.reshape(row_count, col_count)
    rows_wide = rows_scaled.astype(jnp.float32)
    cols_wide = cols_scaled.astype(jnp.float32)
    rows_sq = jnp.sum(rows_wide * rows_wide, axis=1)
    cols_sq = jnp.sum(cols_wide * cols_wide, axis=1)
    part_scaled = rows_scaled
    part_sq = rows_sq
    part_ab = tile
    part = kernel_weights(part_scaled, part_sq, cols_scaled, cols_sq, part_ab)
    own = rows_wide
    total = jnp.sum(part, axis=1, dtype=jnp.float32)
    first = sent_and_summed(
        (
            total[:, None] * own - jnp.dot(part, cols_scaled, preferred_element_type=jnp.float32)
        ).astype(jnp.bfloat16),
        "col",
        0,
    )
    part_scaled = cols_scaled
    part_sq = cols_sq
    part_ab = tile
    part = kernel_weights(rows_scaled, rows_sq, part_scaled, part_sq, part_ab)
    own = cols_wide
    total = jnp.sum(part, axis=0, dtype=jnp.float32)
    product = lax.dot_general(
        part, rows_scaled, (((0,), (0,)), ((), ())), preferred_element_type=jnp.float32
    )
    second = sent_and_summed((total[:, None] * own - product).astype(jnp.bfloat16), "row", 0)
    return -(first + second) * inv_scale[None, :]


def solution(mesh):
    placed = (P(("row", "col"), None), P("row", None, "col", None), P())
    return jax.shard_map(
        per_device, mesh=mesh, in_specs=placed, out_specs=P(("row", "col"), None), check_vma=False
    )
```

profile of v0, /device:TPU:32, one launch (start us, length us, event | category | flops | bytes accessed | tf_op | source)
XLA Modules:
  0.0 100.5 jit_solution(11640922230703904858)
XLA Ops:
  0.0 0.8 multiply_convert_fusion
  0.8 0.9 broadcast_in_dim.2
  1.7 19.4 %all_to_all.20 = bf16[16,128,128]{2,1,0:T(8,128)(2,1)S(1)} all-to-all(bf16[16,128,128]{2,1,0:T(8,128)(2,1)} %broadcast_in_dim.2), channel_id=1, replica_groups=mesh['row'=16,'col'=16] {'row'}, dimensions={0} | all-to-all | bytes 1048576 | tf_op jit(solution)/shard_map/all_to_all | solution.py:9
  21.0 8.7 %all-to-all-start = ((bf16[16,128,128]{2,1,0:T(8,128)(2,1)}), bf16[16,128,128]{2,1,0:T(8,128)(2,1)S(1)}, u32[]{:S(2)}, u32[]{:S(2)}) async-start(bf16[16,128,128]{2,1,0:T(8,128)(2,1)} %broadcast_in_dim.2), calls=%async_computation | async-start | bytes 1048576 | tf_op jit(solution)/shard_map/all_to_all | solution.py:9
  29.7 11.3 %convert.1 = f32[256,8,16,128]{3,2,1,0:T(8,128)} convert(bf16[256,8,16,128]{3,2,1,0:T(8,128)(2,1)} %bitcast.20) | non-fusion elementwise | flops 4194304 | bytes 25165824
  41.0 0.3 multiply_reduce_fusion
  41.4 2.9 %all-to-all-done = bf16[16,128,128]{2,1,0:T(8,128)(2,1)S(1)} async-done(((bf16[16,128,128]{2,1,0:T(8,128)(2,1)}), bf16[16,128,128]{2,1,0:T(8,128)(2,1)S(1)}, u32[]{:S(2)}, u32[]{:S(2)}) %all-to-all-start) | async-done | bytes 524320 | tf_op jit(solution)/shard_map/all_to_all | solution.py:9
  44.3 0.3 multiply_reduce_fusion.1
  44.6 12.8 %convert_reduce_fusion = (f32[2048]{0:T(1024)S(1)}, f32[2048]{0:T(1024)S(1)}, bf16[2048,2048]{1,0:T(8,128)(2,1)S(1)}) fusion(bf16[2048,128]{1,0:T(8,128)(2,1)S(1)} %bitcast.24, bf16[2048,128]{1,0:T(8,128)(2,1)S(1)} %bitcast.21, f32[2048]{0:T(1024)S(1)} %bitcast.27, f32[2048]{0:T(1024)S(1)} %bitcast.28, f32[256,8,16,128]{3,2,1,0:T(8,128)} %convert.1), kind=kOutput, calls=%fused_computation | convolution fusion | flops 1111486464 | bytes 26247168 | tf_op jit(solution)/shard_map/dot_general | solution.py:35
  57.4 0.0 copy-start.1
  57.4 0.0 copy-start
  57.4 3.2 %copy-done.1 = bf16[2048,2048]{1,0:T(8,128)(2,1)} copy-done((bf16[2048,2048]{1,0:T(8,128)(2,1)}, bf16[2048,2048]{1,0:T(8,128)(2,1)S(1)}, u32[]{:S(2)}) %copy-start.1) | copy-done | bytes 8388632
  60.6 3.4 %fusion.2 = bf16[2048,128]{1,0:T(8,128)(2,1)} fusion(bf16[2048,2048]{1,0:T(8,128)(2,1)S(1)} %get-tuple-element.7, bf16[2048,128]{1,0:T(8,128)(2,1)S(1)} %bitcast.25, bf16[2048,128]{1,0:T(8,128)(2,1)S(1)} %bitcast.22, f32[2048]{0:T(1024)S(1)} %get-tuple-element.5), kind=kOutput, calls=%fused_computation.7 | convolution fusion | flops 1074790400 | bytes 9969664 | tf_op jit(solution)/shard_map/dot_general | solution.py:72
  64.0 4.3 %all-to-all-start.3 = ((bf16[16,128,128]{2,1,0:T(8,128)(2,1)}), bf16[16,128,128]{2,1,0:T(8,128)(2,1)S(1)}, u32[]{:S(2)}, u32[]{:S(2)}) async-start(bf16[16,128,128]{2,1,0:T(8,128)(2,1)} %bitcast.5), calls=%async_computation.3 | async-start | bytes 1048576 | tf_op jit(solution)/shard_map/all_to_all | solution.py:30
  68.4 6.6 %fusion.1 = bf16[2048,128]{1,0:T(8,128)(2,1)} fusion(bf16[2048,2048]{1,0:T(8,128)(2,1)} %copy-done.1, bf16[2048,128]{1,0:T(8,128)(2,1)S(1)} %bitcast.23, bf16[2048,128]{1,0:T(8,128)(2,1)S(1)} %bitcast.26, f32[2048]{0:T(1024)S(1)} %get-tuple-element.6), kind=kOutput, calls=%fused_computation.6 | convolution fusion | flops 1074790400 | bytes 9969664 | tf_op jit(solution)/shard_map/dot_general | solution.py:61
  74.9 5.8 %all-to-all-done.3 = bf16[16,128,128]{2,1,0:T(8,128)(2,1)S(1)} async-done(((bf16[16,128,128]{2,1,0:T(8,128)(2,1)}), bf16[16,128,128]{2,1,0:T(8,128)(2,1)S(1)}, u32[]{:S(2)}, u32[]{:S(2)}) %all-to-all-start.3) | async-done | bytes 524320 | tf_op jit(solution)/shard_map/all_to_all | solution.py:30
  80.7 4.6 %all-to-all-start.2 = ((bf16[16,128,128]{2,1,0:T(8,128)(2,1)}), bf16[16,128,128]{2,1,0:T(8,128)(2,1)S(1)}, u32[]{:S(2)}, u32[]{:S(2)}) async-start(bf16[16,128,128]{2,1,0:T(8,128)(2,1)} %bitcast.4), calls=%async_computation.2 | async-start | bytes 1048576 | tf_op jit(solution)/shard_map/all_to_all | solution.py:30
  85.3 0.1 convert_reduce_fusion.2
  85.4 14.5 %all-to-all-done.2 = bf16[16,128,128]{2,1,0:T(8,128)(2,1)S(1)} async-done(((bf16[16,128,128]{2,1,0:T(8,128)(2,1)}), bf16[16,128,128]{2,1,0:T(8,128)(2,1)S(1)}, u32[]{:S(2)}, u32[]{:S(2)}) %all-to-all-start.2) | async-done | bytes 524320 | tf_op jit(solution)/shard_map/all_to_all | solution.py:30
  99.8 0.1 convert_reduce_fusion.3
  99.9 0.0 copy-done
  99.9 0.6 negate_multiply_fusion
Async XLA Ops:
  21.0 23.2 %all-to-all-start = ((bf16[16,128,128]{2,1,0:T(8,128)(2,1)}), bf16[16,128,128]{2,1,0:T(8,128)(2,1)S(1)}, u32[]{:S(2)}, u32[]{:S(2)}) async-start(bf16[16,128,128]{2,1,0:T(8,128)(2,1)} %broadcast_in_dim.2), calls=%async_computation | async-start | bytes 1048576 | tf_op jit(solution)/shard_map/all_to_all | solution.py:9
  57.4 3.2 %copy-start.1 = (bf16[2048,2048]{1,0:T(8,128)(2,1)}, bf16[2048,2048]{1,0:T(8,128)(2,1)S(1)}, u32[]{:S(2)}) copy-start(bf16[2048,2048]{1,0:T(8,128)(2,1)S(1)} %get-tuple-element.7) | copy-start | bytes 25165828
  57.4 42.5 %copy-start = (f32[128]{0:T(128)S(1)}, f32[128]{0:T(128)}, u32[]{:S(2)}) copy-start(f32[128]{0:T(128)} %param.5) | copy-start | bytes 1540
  64.0 16.6 %all-to-all-start.3 = ((bf16[16,128,128]{2,1,0:T(8,128)(2,1)}), bf16[16,128,128]{2,1,0:T(8,128)(2,1)S(1)}, u32[]{:S(2)}, u32[]{:S(2)}) async-start(bf16[16,128,128]{2,1,0:T(8,128)(2,1)} %bitcast.5), calls=%async_computation.3 | async-start | bytes 1048576 | tf_op jit(solution)/shard_map/all_to_all | solution.py:30
  80.7 19.1 %all-to-all-start.2 = ((bf16[16,128,128]{2,1,0:T(8,128)(2,1)}), bf16[16,128,128]{2,1,0:T(8,128)(2,1)S(1)}, u32[]{:S(2)}, u32[]{:S(2)}) async-start(bf16[16,128,128]{2,1,0:T(8,128)(2,1)} %bitcast.4), calls=%async_computation.2 | async-start | bytes 1048576 | tf_op jit(solution)/shard_map/all_to_all | solution.py:30
where the time goes:
time: 101 us
  waiting for transfers between devices  23.1 us (23%)
  matrix products  22.8 us (23%)
  blocking collectives  19.4 us (19%)
  starting transfers between devices  17.6 us (17%)
  other arithmetic  13.5 us (13%)
  local copies, waits for them, and re-layouts  4.1 us (4%)
    all_to_all x2, waiting for transfers between devices, sent_and_summed(): lax.all_to_all(parts, axis, split_axis=0, concat_axis=0, tiled=True)  20.2 us
    all_to_all x1, blocking collectives, from_everyone(): return lax.all_to_all(copies, axis, split_axis=0, concat_axis=0, tiled=True)  19.4 us
    dot_general x1, matrix products, kernel_weights(): lax.dot_general(left_scaled, right_scaled, (((1,), (1,)), ((), ())), pref...  12.8 us
    unnamed x1, other arithmetic  11.3 us
    all_to_all x2, starting transfers between devices, sent_and_summed(): lax.all_to_all(parts, axis, split_axis=0, concat_axis=0, tiled=True)  8.9 us
    all_to_all x1, starting transfers between devices, from_everyone(): return lax.all_to_all(copies, axis, split_axis=0, concat_axis=0, tiled=True)  8.7 us
    dot_general x1, matrix products, per_device(): jnp.dot(part, cols_scaled, preferred_element_type=jnp.float32)  6.58 us
    dot_general x1, matrix products, per_device(): lax.dot_general(part, rows_scaled, (((0,), (0,)), ((), ())), preferred_el...  3.42 us
  transfers between devices with their start and end apart: 3, of which 3 were waited for; matrix products, arithmetic and copies ran while one was open for 18% of the time, Pallas kernels for 0%

commit v1 on v0

v1 whole, which is shorter than its diff:
```python
import functools

import jax
import jax.numpy as jnp
from jax import lax
from jax.experimental import pallas as pl
from jax.experimental.pallas import tpu as pltpu
from jax.sharding import PartitionSpec as P

f32, bf16 = jnp.float32, jnp.bfloat16
B = 128
N = 2048
MESH = pl.DeviceIdType.MESH
ZORDER = (0, 1, -1, 2, -2, 3, -3, 4)
ZSLOT = {d % 8: k for k, d in enumerate(ZORDER)}
PLANE = ((0, 0), (1, 0), (3, 0), (0, 1), (2, 0), (1, 1), (3, 1), (2, 1))
PSLOT = {d: k for k, d in enumerate(PLANE)}


def split3(h):
    hi = h.astype(bf16)
    rest = h - hi.astype(f32)
    mid = rest.astype(bf16)
    return hi.astype(f32), mid.astype(f32), (rest - mid.astype(f32)).astype(bf16).astype(f32)


def kernel(
    points, abar, inv_scale, out,
    rows_raw, cols_raw, inv, tile, flat, left, right_t, right, left_t, weights, prods, second_t,
    y_out, y_in, z_out, z_in, d_out, d_in, p_out, p_in, result,
    load_sem, tile_sem,
    rz_send, rz_recv, ry_send, ry_recv, cp_send, cp_recv, cd_send, cd_recv,
    y_send, y_recv, z_send, z_recv, d_send, d_recv, p_send, p_recv,
):
    row, col = lax.axis_index("row"), lax.axis_index("col")
    x, y_hi, core = row // 4, (row // 2) % 2, row % 2
    y_lo, z = col // 8, col % 8

    def at_z(d):
        return (row, y_lo * 8 + (z + d + 8) % 8)

    def plane_row(d, which):
        return ((x + d[0]) % 4) * 4 + ((y_hi + d[1]) % 2) * 2 + which

    def at_plane(d):
        return (plane_row(d, core), col)

    at_y = (row, (1 - y_lo) * 8 + z)
    at_core = (row + 1 - 2 * core, col)

    peers = [at_core, at_y] + [at_z(d) for d in ZORDER[1:]] + [at_plane(d) for d in PLANE[1:]]
    barrier = pltpu.get_barrier_semaphore()
    for peer in reversed(peers):
        pl.semaphore_signal(barrier, inc=1, device_id=peer, device_id_type=MESH)

    loads = [
        pltpu.make_async_copy(points, rows_raw.at[0], load_sem.at[0]),
        pltpu.make_async_copy(points, cols_raw.at[row], load_sem.at[1]),
        pltpu.make_async_copy(inv_scale, inv, load_sem.at[2]),
    ]
    for load in loads:
        load.start()

    def tile_rows(k):
        zk = (z + ZORDER[k] + 8) % 8
        return [(h * 8 + zk) * B for h in (y_lo, 1 - y_lo)]

    tiles = []
    for k in range(8):
        for h, start in enumerate(tile_rows(k)):
            tiles.append(
                pltpu.make_async_copy(
                    abar.at[pl.ds(start, B)],
                    tile.at[pl.ds((2 * k + h) * B, B)],
                    tile_sem.at[2 * k + h],
                )
            )
    for copy in tiles:
        copy.start()
    for load in loads:
        load.wait()

    def relayout(s):
        tiles[s].wait()

        def group(g, carry):
            at = pl.ds(pl.multiple_of(s * B + g * 16, 16), 16)
            turned = pltpu.einshape("iap->aip", tile[at])
            for a in range(16):
                flat[at, a * B : (a + 1) * B] = turned[a]
            return carry

        lax.fori_loop(0, B // 16, group, 0, unroll=2)

    for s in range(6):
        relayout(s)

    pl.semaphore_wait(barrier, len(peers))

    def remote(src, dst, send, recv, peer):
        return pltpu.make_async_remote_copy(
            src_ref=src, dst_ref=dst, send_sem=send, recv_sem=recv, device_id=peer, device_id_type=MESH
        )

    to_plane = {
        k: remote(cols_raw.at[row], cols_raw.at[row], cp_send.at[k], cp_recv.at[PSLOT[(-d[0]) % 4, d[1]]], at_plane(d))
        for k, d in enumerate(PLANE)
        if k
    }
    from_plane = {
        k: remote(cols_raw.at[row], cols_raw.at[plane_row(d, core)], cp_send.at[k], cp_recv.at[k], at_plane(d))
        for k, d in enumerate(PLANE)
        if k
    }
    to_core = {
        k: remote(
            cols_raw.at[plane_row(d, core)], cols_raw.at[plane_row(d, core)], cd_send.at[k], cd_recv.at[k], at_core
        )
        for k, d in enumerate(PLANE)
    }
    from_core = {
        k: remote(
            cols_raw.at[plane_row(d, core)], cols_raw.at[plane_row(d, 1 - core)], cd_send.at[k], cd_recv.at[k], at_core
        )
        for k, d in enumerate(PLANE)
    }
    to_z = {
        k: remote(rows_raw.at[0], rows_raw.at[2 * ZSLOT[(-d) % 8]], rz_send.at[k], rz_recv.at[ZSLOT[(-d) % 8]], at_z(d))
        for k, d in enumerate(ZORDER)
        if k
    }
    from_z = {
        k: remote(rows_raw.at[0], rows_raw.at[2 * k], rz_send.at[k], rz_recv.at[k], at_z(ZORDER[k]))
        for k in range(1, 8)
    }
    to_y = {
        k: remote(rows_raw.at[2 * k], rows_raw.at[2 * k + 1], ry_send.at[k], ry_recv.at[k], at_y) for k in range(8)
    }
    to_core[0].start()
    for k in range(1, 8):
        to_plane[k].start()
    to_y[0].start()
    for k in range(1, 8):
        to_z[k].start()

    scale = inv[...]
    lane = lax.broadcasted_iota(jnp.int32, (B, B), 1)
    sub = lax.broadcasted_iota(jnp.int32, (B, B), 0)

    def prepare_row(s):
        at = pl.ds(pl.multiple_of(s * B, B), B)
        scaled = (rows_raw[s].astype(f32) * scale).astype(bf16)
        wide = scaled.astype(f32)
        hi, mid, low = split3(jnp.broadcast_to(-0.5 * jnp.sum(wide * wide, axis=1, keepdims=True), (B, B)))
        extra = jnp.where(
            lane == 0, hi, jnp.where(lane == 1, mid, jnp.where(lane == 2, low, jnp.where(lane < 6, 1.0, 0.0)))
        )
        left[at, :B] = scaled
        left[at, B:] = extra.astype(bf16)
        left_t[:B, at] = wide.T.astype(bf16)
        left_t[B:, at] = jnp.ones((16, B), bf16)

    def prepare_col(a):
        at = pl.ds(pl.multiple_of(a * B, B), B)
        scaled = (cols_raw[a].astype(f32) * scale).astype(bf16)
        right[at, :B] = scaled
        right[at, B:] = jnp.ones((B, B), bf16)
        wide = scaled.astype(f32).T
        hi, mid, low = split3(jnp.broadcast_to(-0.5 * jnp.sum(wide * wide, axis=0, keepdims=True), (B, B)))
        extra = jnp.where(
            sub < 3,
            1.0,
            jnp.where(sub == 3, hi, jnp.where(sub == 4, mid, jnp.where(sub == 5, low, 0.0))),
        )
        right_t[:B, at] = wide.astype(bf16)
        right_t[B:, at] = extra.astype(bf16)

    prepare_col(row)
    prepare_row(0)
    for s in range(6, 16):
        relayout(s)

    for k in (1, 2):
        from_plane[k].wait_recv()
        to_core[k].start()
        from_z[k].wait_recv()
        to_y[k].start()
    for k in range(3, 8):
        from_plane[k].wait_recv()
        to_core[k].start()
    for k in range(1, 8):
        prepare_col(plane_row(PLANE[k], core))
    for k in range(8):
        from_core[k].wait_recv()
        prepare_col(plane_row(PLANE[k], 1 - core))
    to_y[0].wait_recv()
    prepare_row(1)

    second_t[...] = jnp.zeros_like(second_t)

    y_sends = {k: remote(y_out.at[k], y_in.at[k], y_send.at[k], y_recv.at[k], at_y) for k in range(8)}
    z_sends = {
        k: remote(z_out.at[k], z_in.at[ZSLOT[(-d) % 8]], z_send.at[k], z_recv.at[ZSLOT[(-d) % 8]], at_z(d))
        for k, d in enumerate(ZORDER)
        if k
    }
    z_arrive = {
        k: remote(z_out.at[k], z_in.at[k], z_send.at[k], z_recv.at[k], at_z(ZORDER[k])) for k in range(1, 8)
    }

    def first_terms(s):
        at = pl.ds(s * B, B)
        both = prods[at, :]
        return both[:, B:] * left[at, :B].astype(f32) - both[:, :B]

    def give_y(k):
        y_out[k] = first_terms(2 * k + 1).astype(bf16)

    def give_z(k):
        y_sends[k].wait_recv()
        z_out[k] = (first_terms(2 * k) + y_in[k].astype(f32)).astype(bf16)

    step_cols = 256
    for t in range(9):
        slot = t % 2
        if 3 <= t + 2 < 8:
            from_z[t + 2].wait_recv()
            to_y[t + 2].start()
        if 0 < t < 8:
            to_y[t].wait_recv()
            prepare_row(2 * t)
            prepare_row(2 * t + 1)
        at = pl.ds(t * 2 * B, 2 * B)
        before = pl.ds((t - 1) * 2 * B, 2 * B)
        total = None
        for c in range(N // step_cols):
            cs = slice(c * step_cols, (c + 1) * step_cols)
            if t < 8:
                power = jnp.dot(left[at, :], right_t[:, cs], preferred_element_type=f32)
                weights[slot, :, cs] = (flat[at, cs].astype(f32) * jnp.exp(power)).astype(bf16)
            if t > 0:
                held = weights[1 - slot, :, cs]
                part = jnp.dot(held, right[cs, :], preferred_element_type=f32)
                total = part if total is None else total + part
                second_t[:, cs] += jnp.dot(left_t[:, before], held, preferred_element_type=f32)
        if t > 0:
            prods[before, :] = total
        if t >= 2:
            y_sends[t - 2].start()
        if t >= 1:
            give_y(t - 1)
        if t >= 6 and t - 5 >= 1:
            z_sends[t - 5].start()
        if t >= 5 and t - 4 >= 1:
            give_z(t - 4)

    d_sends = {k: remote(d_out.at[k], d_in.at[k], d_send.at[k], d_recv.at[k], at_core) for k in range(8)}
    p_sends = {
        k: remote(p_out.at[k], p_in.at[PSLOT[(-d[0]) % 4, d[1]]], p_send.at[k], p_recv.at[PSLOT[(-d[0]) % 4, d[1]]], at_plane(d))
        for k, d in enumerate(PLANE)
        if k
    }
    p_arrive = {
        k: remote(p_out.at[k], p_in.at[k], p_send.at[k], p_recv.at[k], at_plane(PLANE[k])) for k in range(1, 8)
    }

    def second_terms(a):
        at = pl.ds(pl.multiple_of(a * B, B), B)
        return second_t[B : B + 1, at] * right_t[:B, at].astype(f32) - second_t[:B, at]

    for k in reversed(range(8)):
        d_out[k] = second_terms(plane_row(PLANE[k], 1 - core)).astype(bf16)
        if k < 7:
            d_sends[k + 1].start()
    d_sends[0].start()
    y_sends[7].start()
    z_sends[4].start()
    for k in reversed(range(1, 8)):
        d_sends[k].wait_recv()
        p_out[k] = (second_terms(plane_row(PLANE[k], core)) + d_in[k].astype(f32)).astype(bf16)
        if k < 7:
            p_sends[k + 1].start()
    d_sends[0].wait_recv()
    mine_t = second_terms(row) + d_in[0].astype(f32)
    p_sends[1].start()
    for k in (5, 6, 7):
        give_z(k)
        if k > 5:
            z_sends[k - 1].start()
    y_sends[0].wait_recv()
    mine = first_terms(0) + y_in[0].astype(f32)
    z_sends[7].start()
    for k in range(1, 8):
        p_arrive[k].wait_recv()
        mine_t += p_in[k].astype(f32)
    mine += mine_t.T
    for k in range(1, 8):
        z_arrive[k].wait_recv()
        mine += z_in[k].astype(f32)
    result[...] = -mine * scale
    store = pltpu.make_async_copy(result, out, load_sem.at[0])
    store.start()

    for group in (to_plane, to_core, to_z, to_y, y_sends, z_sends, d_sends, p_sends):
        for copy in group.values():
            copy.wait_send()
    store.wait()


def per_device(points, abar, inv_scale):
    vmem, dma = pltpu.VMEM, pltpu.SemaphoreType.DMA
    blocks = lambda n: vmem((n, B, B), bf16)
    return pl.pallas_call(
        kernel,
        out_shape=jax.ShapeDtypeStruct((B, B), f32),
        in_specs=[pl.BlockSpec(memory_space=pl.ANY)] * 3,
        out_specs=pl.BlockSpec(memory_space=pl.ANY),
        scratch_shapes=[
            blocks(16), blocks(16), vmem((1, B), f32),
            vmem((N, 16, B), bf16), vmem((N, N), bf16),
            vmem((N, 2 * B), bf16), vmem((2 * B, N), bf16), vmem((N, 2 * B), bf16), vmem((B + 16, N), bf16),
            vmem((2, 2 * B, N), bf16), vmem((N, 2 * B), f32), vmem((B + 16, N), f32),
            blocks(8), blocks(8), blocks(8), blocks(8), blocks(8), blocks(8), blocks(8), blocks(8),
            vmem((B, B), f32),
            dma((3,)), dma((16,)),
            *[dma((8,)) for _ in range(16)],
        ],
        compiler_params=pltpu.CompilerParams(
            collective_id=0, has_side_effects=True, vmem_limit_bytes=60 * 2**20
        ),
    )(points, abar.reshape(N, 16, B), inv_scale.reshape(1, B))


def solution(mesh):
    placed = (P(("row", "col"), None), P("row", None, "col", None), P())
    return jax.shard_map(
        per_device, mesh=mesh, in_specs=placed, out_specs=P(("row", "col"), None), check_vma=False
    )
```

time: 101 us -> 44.3 us (0.44)
  the two profiles are of different devices: /device:TPU:32 before, /device:TPU:2 now
where the time goes in v1:
time: 44.3 us; the launch traced here: 44.1 us
  Pallas kernels  42.7 us (96%)
  local copies, waits for them, and re-layouts  1.47 us (3%)
    pallas_call x1, Pallas kernels, per_device(): pl.pallas_call(kernel, out_shape=jax.ShapeDtypeStruct((B, B), f32), in_sp...  42.7 us
    unnamed x1, local copies, waits for them, and re-layouts  1.47 us

profile of v1, /device:TPU:2, one launch (start us, length us, event | category | flops | bytes accessed | tf_op | source)
XLA Modules:
  0.0 44.1 jit_solution(6774589623325505641)
XLA Ops:
  0.0 42.7 %shard_map.37 = f32[128,128]{1,0:T(8,128)} custom-call(bf16[128,128]{1,0:T(8,128)(2,1)} %points.1, bf16[2048,16,128]{2,1,0:T(8,128)(2,1)} %bitcast.2, f32[1,128]{1,0:T(1,128)} %bitcast.3), custom_call_target="tpu_custom_call" | custom-call | tf_op jit(solution)/shard_map/pallas_call | solution.py:313
  42.7 1.5 %copy.5 = f32[128,128]{1,0:T(8,128)} copy(f32[128,128]{1,0:T(8,128)} %shard_map.37) | data formatting | bytes 131072

commit v2 on v0

v2 whole, which is shorter than its diff:
```python
import functools

import jax
import jax.numpy as jnp
from jax import lax
from jax.experimental import pallas as pl
from jax.experimental.pallas import tpu as pltpu
from jax.sharding import PartitionSpec as P

f32, bf16 = jnp.float32, jnp.bfloat16
B = 128
N = 2048
MESH = pl.DeviceIdType.MESH
ZS = (0, 1, -1, 2, -2, 3, -3, 4)
PLANE = ((0, 0), (1, 0), (3, 0), (2, 0), (0, 1), (3, 1), (1, 1), (2, 1))
ACROSS = 4
ZSLOT = {d % 8: k for k, d in enumerate(ZS)}
PSLOT = {d: k for k, d in enumerate(PLANE)}
PAIRS = (
    ((2, 0), (-2, 0)),
    ((1, 1), (-1, 1)),
    ((2, 1), (-2, 1)),
    ((3, 0), (-3, 0)),
    ((3, 1), (-3, 1)),
    ((4, 0), (4, 1)),
)
LAST = ((1, 0), (-1, 0), (0, 0), (0, 1))
NEAR = 5
UNITS = (
    (0, 2, 0, NEAR),
    (2, 2, 0, NEAR),
    (4, 2, 0, NEAR),
    (6, 2, 0, NEAR),
    (0, 4, NEAR, 8),
    (4, 4, NEAR, 8),
    (8, 2, 0, 8),
    (10, 2, 0, 8),
    (12, 4, 6, 8),
    (12, 4, 4, 6),
    (12, 4, 2, 4),
    (12, 4, 0, 2),
)
GROUPS = tuple(g for pair in PAIRS for g in pair) + LAST
POS = {(d % 8, h): i for i, (d, h) in enumerate(GROUPS)}
EARLY = 12
NEXT_P = 2


def split3(h):
    hi = h.astype(bf16)
    rest = h - hi.astype(f32)
    mid = rest.astype(bf16)
    return hi.astype(f32), mid.astype(f32), (rest - mid.astype(f32)).astype(bf16).astype(f32)


def kernel(
    points, abar, inv_scale, out,
    rows_raw, cols_raw, inv, tile, flat, left, right_t, right, left_t, weights, prods, second_t,
    f_out, f_in, d_out, d_in, p_out, p_in,
    load_sem, tile_sem, sent,
    rz_recv, ry_recv, cp_recv, cd_recv, d_recv, p_recv, f_recv,
):
    row, col = lax.axis_index("row"), lax.axis_index("col")
    x, y_hi, core = row // 4, (row // 2) % 2, row % 2
    y_lo, z = col // 8, col % 8

    def at_z(d):
        return (row, y_lo * 8 + (z + d + 8) % 8)

    def plane_row(k, which):
        d = PLANE[k]
        return ((x + d[0]) % 4) * 4 + ((y_hi + d[1]) % 2) * 2 + which

    def at_plane(k):
        return (plane_row(k, core), col)

    at_y = (row, (1 - y_lo) * 8 + z)
    at_core = (row + 1 - 2 * core, col)

    peers = [at_core, at_y] + [at_z(d) for d in (1, -1, 2, -2)] + [at_plane(k) for k in (1, 2, 3, 4)]
    barrier = pltpu.get_barrier_semaphore()
    for peer in reversed(peers):
        pl.semaphore_signal(barrier, inc=1, device_id=peer, device_id_type=MESH)

    own = POS[0, 0]
    loads = [
        pltpu.make_async_copy(points, rows_raw.at[own], load_sem.at[0]),
        pltpu.make_async_copy(points, cols_raw.at[0], load_sem.at[1]),
        pltpu.make_async_copy(inv_scale, inv, load_sem.at[2]),
    ]
    for load in loads:
        load.start()
    with jax.named_scope("loads"):
        for load in loads:
            load.wait()

    tiles = []
    for s, (d, h) in enumerate(GROUPS):
        start = ((y_lo if h == 0 else 1 - y_lo) * 8 + (z + d + 8) % 8) * B
        tiles.append(pltpu.make_async_copy(abar.at[pl.ds(start, B)], tile.at[pl.ds(s * B, B)], tile_sem.at[s]))
    for copy in tiles:
        copy.start()

    with jax.named_scope("barrier"):
        pl.semaphore_wait(barrier, len(peers))

    n_sent = []

    def remote(src, dst, recv, peer):
        return pltpu.make_async_remote_copy(
            src_ref=src, dst_ref=dst, send_sem=sent, recv_sem=recv, device_id=peer, device_id_type=MESH
        )

    def start(copy):
        n_sent.append(1)
        copy.start()

    def opposite(k):
        d = PLANE[k]
        return PSLOT[(-d[0]) % 4, d[1]]

    to_plane = {
        k: remote(
            cols_raw.at[0 if k <= ACROSS else 2 * ACROSS],
            cols_raw.at[2 * opposite(k)],
            cp_recv.at[opposite(k)],
            at_plane(k if k <= ACROSS else PSLOT[PLANE[k][0], 0]),
        )
        for k in range(1, 8)
    }
    from_plane = {
        k: remote(cols_raw.at[0], cols_raw.at[2 * k], cp_recv.at[k], at_plane(1)) for k in range(1, 8)
    }
    to_core = {
        k: remote(cols_raw.at[2 * k], cols_raw.at[2 * k + 1], cd_recv.at[k], at_core) for k in range(8)
    }
    to_z = {
        d: remote(rows_raw.at[own], rows_raw.at[POS[-d % 8, 0]], rz_recv.at[ZSLOT[-d % 8]], at_z(d))
        for d in (1, -1, 2, -2)
    }
    for d in (3, -3):
        step = d // 3
        to_z[d] = remote(
            rows_raw.at[POS[-2 * step % 8, 0]], rows_raw.at[POS[-d % 8, 0]], rz_recv.at[ZSLOT[-d % 8]], at_z(step)
        )
    to_z[4] = remote(
        rows_raw.at[jnp.where(core == 0, POS[-2 % 8, 0], POS[2, 0])],
        rows_raw.at[POS[4, 0]],
        rz_recv.at[ZSLOT[4]],
        at_z(2 - 4 * core),
    )
    from_z = {
        d: remote(rows_raw.at[own], rows_raw.at[POS[d % 8, 0]], rz_recv.at[ZSLOT[d % 8]], at_z(1)) for d in ZS[1:]
    }
    to_y = {
        d: remote(rows_raw.at[POS[d % 8, 0]], rows_raw.at[POS[d % 8, 1]], ry_recv.at[ZSLOT[d % 8]], at_y) for d in ZS
    }
    start(to_core[0])
    for k in (4, 3, 1, 2):
        start(to_plane[k])
    start(to_y[0])
    for d in (1, -1, 2, -2):
        start(to_z[d])

    scale = inv[...]
    lane = lax.broadcasted_iota(jnp.int32, (B, B), 1)
    sub = lax.broadcasted_iota(jnp.int32, (16, B), 0)

    def prepare_row(s):
        at = pl.ds(s * B, B)
        scaled = (rows_raw[s].astype(f32) * scale).astype(bf16)
        wide = scaled.astype(f32)
        hi, mid, low = split3(jnp.broadcast_to(-0.5 * jnp.sum(wide * wide, axis=1, keepdims=True), (B, B)))
        extra = jnp.where(
            lane == 0, hi, jnp.where(lane == 1, mid, jnp.where(lane == 2, low, jnp.where(lane < 6, 1.0, 0.0)))
        )
        left[at, :B] = scaled
        left[at, B:] = extra.astype(bf16)
        left_t[:B, at] = wide.T.astype(bf16)
        left_t[B:, at] = jnp.ones((16, B), bf16)

    def prepare_col(a):
        at = pl.ds(a * B, B)
        scaled = (cols_raw[a].astype(f32) * scale).astype(bf16)
        right[at, :B] = scaled
        right[at, B:] = jnp.ones((B, B), bf16)
        wide = scaled.astype(f32).T
        hi, mid, low = split3(jnp.broadcast_to(-0.5 * jnp.sum(wide * wide, axis=0, keepdims=True), (16, B)))
        extra = jnp.where(
            sub < 3,
            1.0,
            jnp.where(sub == 3, hi, jnp.where(sub == 4, mid, jnp.where(sub == 5, low, 0.0))),
        )
        right_t[:B, at] = wide.astype(bf16)
        right_t[B : B + 16, at] = extra.astype(bf16)
        right_t[B + 16 :, at] = jnp.zeros((B - 16, B), bf16)

    places = []
    for a in range(16):
        dx, dy = (a // 4 - x + 4) % 4, (a // 2 % 2 - y_hi + 2) % 2
        k = jnp.int32(0)
        for i, d in enumerate(PLANE):
            k = jnp.where((dx == d[0]) & (dy == d[1]), i, k)
        places.append(pl.multiple_of((2 * k + (a % 2 - core + 2) % 2) * B, B))

    def relayout(s):
        tiles[s].wait()

        def group(g, carry):
            at = pl.ds(pl.multiple_of(s * B + g * 16, 16), 16)
            turned = pltpu.einshape("iap->aip", tile[at])
            for a in range(16):
                flat[at, pl.ds(places[a], B)] = turned[a]
            return carry

        lax.fori_loop(0, B // 16, group, 0, unroll=2)

    def arrive_z(d):
        with jax.named_scope(f"z_{d}"):
            from_z[d].wait_recv()
        start(to_y[d])

    def arrive_plane(k):
        with jax.named_scope(f"plane_{k}"):
            from_plane[k].wait_recv()
        start(to_core[k])

    with jax.named_scope("relayout"):
        prepare_col(0)
        prepare_row(own)
        for s in range(EARLY):
            relayout(s)
    arrive_plane(ACROSS)
    for k in (7, 6, 5):
        start(to_plane[k])
    for d in (1, -1):
        arrive_z(d)
    with jax.named_scope("relayout2"):
        for s in range(EARLY, 16):
            relayout(s)
    for d in (2, -2):
        arrive_z(d)
    for d in (3, -3, 4):
        start(to_z[d])
    for k in (1, 2, 3):
        arrive_plane(k)
    for k in range(1, NEAR):
        prepare_col(2 * k)
    def from_core(chips):
        with jax.named_scope(f"core_{chips[0]}"):
            for k in chips:
                to_core[k].wait_recv()
        for k in chips:
            prepare_col(2 * k + 1)

    from_core(range(NEAR))

    def f_place(g):
        d, h = g
        if h and d in (3, -3, 4):
            return (row, (1 - y_lo) * 8 + (z + d + 8) % 8)
        return at_z(d) if d else at_y

    f_sends = {
        g: remote(f_out.at[POS[g[0] % 8, g[1]]], f_in.at[POS[-g[0] % 8, g[1]]], f_recv.at[POS[-g[0] % 8, g[1]]], f_place(g))
        for g in GROUPS
        if g != (0, 0)
    }
    f_arrive = {
        g: remote(f_out.at[POS[g[0] % 8, g[1]]], f_in.at[POS[g[0] % 8, g[1]]], f_recv.at[POS[g[0] % 8, g[1]]], at_y)
        for g in GROUPS
        if g != (0, 0)
    }
    d_sends = {k: remote(d_out.at[k], d_in.at[k], d_recv.at[k], at_core) for k in range(8)}
    p_sends = {
        k: remote(
            p_out.at[k],
            p_in.at[opposite(k)],
            p_recv.at[opposite(k)],
            at_plane(k),
        )
        for k in range(1, 8)
    }
    p_arrive = {k: remote(p_out.at[k], p_in.at[k], p_recv.at[k], at_plane(1)) for k in range(1, 8)}

    def first_terms(s):
        both = prods[pl.ds(s * B, B), :]
        return both[:, B:] * left[pl.ds(s * B, B), :B].astype(f32) - both[:, :B]

    def arrived(g):
        with jax.named_scope(f"f_{g[0]}_{g[1]}"):
            f_arrive[g].wait_recv()
        return f_in[POS[g[0] % 8, g[1]]].astype(f32)

    def give_first(g):
        s = POS[g[0] % 8, g[1]]
        terms = first_terms(s)
        if g == (0, 1):
            for d in (1, -1, 2, -2):
                terms += arrived((d, 1))
        f_out[s] = terms.astype(bf16)
        pending.append(f_sends[g])

    def second_terms(a):
        at = pl.ds(a * B, B)
        return second_t[B : B + 1, at] * right_t[:B, at].astype(f32) - second_t[:B, at]

    def weigh(rows, cs):
        power = jnp.dot(left[rows, :], right_t[:, cs], preferred_element_type=f32)
        return (flat[rows, cs].astype(f32) * jnp.exp(power)).astype(bf16)

    def make_weights(u):
        first, n, low, high = UNITS[u]
        rows = pl.ds(first * B, n * B)
        for c in range(low, high):
            cs = slice(c * 2 * B, (c + 1) * 2 * B)
            weights[u % 2, : n * B, cs] = weigh(rows, cs)

    seen_rows, seen_cols = set(), set()

    def use_weights(u):
        first, n, low, high = UNITS[u]
        rows, cs = pl.ds(first * B, n * B), slice(low * 2 * B, high * 2 * B)
        held = weights[u % 2, : n * B, cs]
        part = jnp.dot(held, right[cs, :], preferred_element_type=f32)
        for at, new in ((slice(i * B, (i + 1) * B), first + i) for i in range(n)):
            to = pl.ds(new * B, B)
            if new in seen_rows:
                prods[to, :] += part[at]
            else:
                prods[to, :] = part[at]
            seen_rows.add(new)
        term = jnp.dot(left_t[:, rows], held, preferred_element_type=f32)
        if low in seen_cols:
            second_t[:, cs] += term
        else:
            second_t[:, cs] = term
        seen_cols.update(range(low, high))

    done = {GROUPS[i]: u + 1 for u, (first, n, _, _) in enumerate(UNITS) for i in range(first, first + n)}
    def need(g):
        d, h = g
        if g == (0, 0):
            return
        if h == 1:
            with jax.named_scope(f"y_{d}"):
                to_y[d].wait_recv()

    pending = []

    def flush():
        while pending:
            start(pending.pop(0))

    def give_core(k):
        d_out[k] = second_terms(2 * k + 1).astype(bf16)
        pending.append(d_sends[k])

    def give_plane(k):
        with jax.named_scope(f"d_{k}"):
            d_sends[k].wait_recv()
        terms = second_terms(2 * k) + d_in[k].astype(f32)
        p_out[k] = terms.astype(bf16)
        pending.append(p_sends[k])

    p_queue = [7, 6, 5, 4, 3, 2, 1]
    core_done = {}
    ready = {(0, 0)}

    def fresh(u):
        return [g for g in GROUPS[UNITS[u][0] : UNITS[u][0] + UNITS[u][1]] if g not in ready]

    for g in fresh(0):
        need(g)
        prepare_row(POS[g[0] % 8, g[1]])
        ready.add(g)
    for t in range(len(UNITS) + 1):
        flush()
        if t == 2:
            arrive_plane(6)
            arrive_plane(5)
            arrive_z(3)
            arrive_z(-3)
        if t == 3:
            arrive_plane(7)
            for k in range(NEAR, 8):
                prepare_col(2 * k)
        if t == 4:
            arrive_z(4)
            from_core(range(NEAR, 8))
        nexts = fresh(t + 1) if t + 1 < len(UNITS) else ()
        for g in nexts:
            need(g)
        if t < len(UNITS):
            make_weights(t)
        for g in nexts:
            prepare_row(POS[g[0] % 8, g[1]])
            ready.add(g)
        if t > 0:
            use_weights(t - 1)
        if t > 0 and UNITS[t - 1][0] == 2 * len(PAIRS):
            for k in reversed(range(*UNITS[t - 1][2:])):
                give_core(k)
                core_done[k] = t
        for g in GROUPS:
            if done[g] == t and t < len(UNITS):
                give_first(g)
        while p_queue and core_done.get(p_queue[0], t) + NEXT_P <= t:
            give_plane(p_queue.pop(0))
    flush()
    for g in ((1, 0), (-1, 0)):
        give_first(g)
        if len(pending) > 1:
            start(pending.pop(0))
    while p_queue and p_queue[0] > 1:
        give_plane(p_queue.pop(0))
        start(pending.pop(0))
    give_first((0, 1))
    start(pending.pop(0))
    give_plane(1)
    flush()
    with jax.named_scope("d_0"):
        d_sends[0].wait_recv()
    mine_t = second_terms(0) + d_in[0].astype(f32)
    mine = first_terms(own)
    flush()
    for k in reversed(range(1, 8)):
        with jax.named_scope(f"p_{k}"):
            p_arrive[k].wait_recv()
        mine_t += p_in[k].astype(f32)
    mine += mine_t.T
    for g in ((2, 0), (-2, 0), (3, 0), (-3, 0), (4, 0), (3, 1), (-3, 1), (4, 1), (1, 0), (-1, 0), (0, 1)):
        mine += arrived(g)
    out[...] = mine
    all_sent = flat.at[pl.ds(0, len(n_sent) * B * B // N)]
    with jax.named_scope("sent"):
        pltpu.make_async_copy(all_sent, all_sent, sent).wait()


def per_device(points, abar, inv_scale):
    vmem, dma = pltpu.VMEM, pltpu.SemaphoreType.DMA
    blocks = lambda n: vmem((n, B, B), bf16)
    total = pl.pallas_call(
        kernel,
        out_shape=jax.ShapeDtypeStruct((B, B), f32),
        in_specs=[pl.BlockSpec(memory_space=pltpu.HBM)] * 3,
        out_specs=pl.BlockSpec(memory_space=vmem),
        scratch_shapes=[
            blocks(16), blocks(16), vmem((1, B), f32),
            vmem((N, 16, B), bf16), vmem((N, N), bf16),
            vmem((N, 2 * B), bf16), vmem((2 * B, N), bf16), vmem((N, 2 * B), bf16), vmem((B + 16, N), bf16),
            vmem((2, 4 * B, N), bf16), vmem((N, 2 * B), f32), vmem((B + 16, N), f32),
            blocks(16), blocks(16), *[blocks(8) for _ in range(4)],
            dma((3,)), dma((16,)), dma,
            *[dma((8,)) for _ in range(6)], dma((16,)),
        ],
        compiler_params=pltpu.CompilerParams(
            collective_id=0, has_side_effects=True, vmem_limit_bytes=40 * 2**20
        ),
    )(*[pltpu.with_memory_space_constraint(v, pltpu.HBM) for v in (points, abar.reshape(N, 16, B), inv_scale.reshape(1, B))])
    return -total * inv_scale[None, :]


def solution(mesh):
    placed = (P(("row", "col"), None), P("row", None, "col", None), P())
    return jax.shard_map(
        per_device, mesh=mesh, in_specs=placed, out_specs=P(("row", "col"), None), check_vma=False
    )
```

time: 101 us -> 36.1 us (0.36)
  Pallas kernels: 0 us -> 35.3 us
  waiting for transfers between devices: 23.1 us -> 0 us
  matrix products: 22.8 us -> 0 us
  blocking collectives: 19.4 us -> 0 us
  starting transfers between devices: 17.6 us -> 0 us
  other arithmetic: 13.5 us -> 0.64 us
  local copies, waits for them, and re-layouts: 4.1 us -> 0.01 us
    pallas_call x0 -> x1, Pallas kernels: none -> 35.3 us  [per_device(): pl.pallas_call(kernel, out_shape=jax.ShapeDtypeStruct((B, B), f32), in_sp...]
    all_to_all x3 -> x0, waiting for transfers between devices: 23.1 us -> none  [the longest x2 20.2 us: sent_and_summed(): lax.all_to_all(parts, axis, split_axis=0, concat_axis=0, tiled=True)]
    dot_general x3 -> x0, matrix products: 22.8 us -> none  [the longest x1 12.8 us: kernel_weights(): lax.dot_general(left_scaled, right_scaled, (((1,), (1,)), ((), ())), pref...]
    all_to_all x1 -> x0, blocking collectives: 19.4 us -> none  [from_everyone(): return lax.all_to_all(copies, axis, split_axis=0, concat_axis=0, tiled=True)]
    all_to_all x3 -> x0, starting transfers between devices: 17.6 us -> none  [the longest x2 8.9 us: sent_and_summed(): lax.all_to_all(parts, axis, split_axis=0, concat_axis=0, tiled=True)]
    unnamed x1 -> x0, other arithmetic: 11.3 us -> none
    unnamed x4 -> x2, local copies, waits for them, and re-layouts: 3.21 us -> 0.01 us
  transfers between devices with their start and end apart: 3 -> 0, of which waited for: 3 -> 0; matrix products, arithmetic and copies ran while one was open for 18% -> 0% of each run, Pallas kernels for 0% -> 0%
where the time goes in v2:
time: 36.1 us; the launch traced here: 36 us
  Pallas kernels  35.3 us (98%)
  other arithmetic  0.64 us (2%)
    pallas_call x1, Pallas kernels, per_device(): pl.pallas_call(kernel, out_shape=jax.ShapeDtypeStruct((B, B), f32), in_sp...  35.3 us

profile of v2, /device:TPU:32, one launch (start us, length us, event | category | flops | bytes accessed | tf_op | source)
XLA Modules:
  0.0 36.0 jit_solution(437472782827308835)
XLA Ops:
  0.0 0.0 copy-start
  0.0 35.3 %shard_map.37 = f32[128,128]{1,0:T(8,128)S(1)} custom-call(bf16[128,128]{1,0:T(8,128)(2,1)} %points.1, bf16[2048,16,128]{2,1,0:T(8,128)(2,1)} %bitcast.2, f32[1,128]{1,0:T(1,128)} %bitcast.3), custom_call_target="tpu_custom_call" | custom-call | tf_op jit(solution)/shard_map/pallas_call | solution.py:443
  35.3 0.0 copy-done
  35.3 0.6 %negate_multiply_fusion = f32[128,128]{1,0:T(8,128)} fusion(f32[128,128]{1,0:T(8,128)S(1)} %shard_map.37, f32[128]{0:T(128)S(1)} %copy-done), kind=kLoop, calls=%fused_computation | loop fusion | flops 32768 | bytes 131584 | tf_op jit(solution)/shard_map/mul | solution.py:461
Async XLA Ops:
  0.0 35.3 %copy-start = (f32[128]{0:T(128)S(1)}, f32[128]{0:T(128)}, u32[]{:S(2)}) copy-start(f32[128]{0:T(128)} %param.5) | copy-start | bytes 1540

commit v3 on v2

--- a/solution.py
+++ b/solution.py
@@ -18,13 +18,14 @@
 PSLOT = {d: k for k, d in enumerate(PLANE)}
 PAIRS = (
     ((2, 0), (-2, 0)),
+    ((0, 1), (1, 0)),
     ((1, 1), (-1, 1)),
     ((2, 1), (-2, 1)),
-    ((3, 0), (-3, 0)),
+    ((4, 0), (4, 1)),
     ((3, 1), (-3, 1)),
-    ((4, 0), (4, 1)),
 )
-LAST = ((1, 0), (-1, 0), (0, 0), (0, 1))
+LAST = ((-1, 0), (0, 0), (3, 0), (-3, 0))
+FAR = (4, 3, -3)
 NEAR = 5
 UNITS = (
     (0, 2, 0, NEAR),
@@ -42,6 +43,33 @@
 )
 GROUPS = tuple(g for pair in PAIRS for g in pair) + LAST
 POS = {(d % 8, h): i for i, (d, h) in enumerate(GROUPS)}
+SETS = (
+    [("load", 0), ("load", 1)],
+    [("inv", 0)],
+    *[[("tile", s) for s in range(i, i + 4)] for i in range(0, 16, 4)],
+    [("plane", 1), ("plane", 2), ("plane", 3)],
+    [("plane", 4)],
+    [("plane", 6), ("plane", 5)],
+    [("plane", 7)],
+    [("core", k) for k in range(NEAR)],
+    [("core", k) for k in range(NEAR, 8)],
+    [("z", 1), ("z", -1)],
+    [("z", 2), ("z", -2)],
+    [("z", 4), ("z", 3), ("z", -3)],
+    [("y", 0)],
+    [("y", 1), ("y", -1)],
+    [("y", 2), ("y", -2)],
+    [("y", 4)],
+    [("y", 3), ("y", -3)],
+    *[[("d", k + 1), ("d", k)] for k in (6, 4, 2, 0)],
+    [("p", k) for k in range(1, 8)],
+    [("f", (d, 1)) for d in (1, -1, 2, -2)],
+    [("f", (4, 1))],
+    [("f", (3, 1)), ("f", (-3, 1))],
+    [("f", (d, 0)) for d in ZS[1:]] + [("f", (0, 1))],
+)
+COPIES = tuple(tuple(c) for c in SETS)
+LATE = (2, 6, 7)
 EARLY = 12
 NEXT_P = 2
 
@@ -57,8 +85,7 @@
     points, abar, inv_scale, out,
     rows_raw, cols_raw, inv, tile, flat, left, right_t, right, left_t, weights, prods, second_t,
     f_out, f_in, d_out, d_in, p_out, p_in,
-    load_sem, tile_sem, sent,
-    rz_recv, ry_recv, cp_recv, cd_recv, d_recv, p_recv, f_recv,
+    sems, sent,
 ):
     row, col = lax.axis_index("row"), lax.axis_index("col")
     x, y_hi, core = row // 4, (row // 2) % 2, row % 2
@@ -82,22 +109,40 @@
     for peer in reversed(peers):
         pl.semaphore_signal(barrier, inc=1, device_id=peer, device_id_type=MESH)
 
+    def sem(kind, which):
+        return sems.at[next(i for i, c in enumerate(COPIES) if (kind, which) in c)]
+
+    waited = set()
+
+    def wait_for(kind, which):
+        i = next(i for i, c in enumerate(COPIES) if (kind, which) in c)
+        if i not in waited:
+            waited.add(i)
+            n = len(COPIES[i])
+            if kind == "inv":
+                held = inv
+            elif kind == "tile":
+                held = tile.at[pl.ds(0, n * B)]
+            else:
+                held = rows_raw.at[pl.ds(0, n)]
+            with jax.named_scope(f"{kind}_{str(which).replace(', ', '_')}"):
+                pltpu.make_async_copy(held, held, sems.at[i]).wait()
+
     own = POS[0, 0]
     loads = [
-        pltpu.make_async_copy(points, rows_raw.at[own], load_sem.at[0]),
-        pltpu.make_async_copy(points, cols_raw.at[0], load_sem.at[1]),
-        pltpu.make_async_copy(inv_scale, inv, load_sem.at[2]),
+        pltpu.make_async_copy(points, rows_raw.at[own], sem("load", 0)),
+        pltpu.make_async_copy(points, cols_raw.at[0], sem("load", 1)),
+        pltpu.make_async_copy(inv_scale, inv, sem("inv", 0)),
     ]
     for load in loads:
         load.start()
-    with jax.named_scope("loads"):
-        for load in loads:
-            load.wait()
+    wait_for("load", 0)
+    wait_for("inv", 0)
 
     tiles = []
     for s, (d, h) in enumerate(GROUPS):
         start = ((y_lo if h == 0 else 1 - y_lo) * 8 + (z + d + 8) % 8) * B
-        tiles.append(pltpu.make_async_copy(abar.at[pl.ds(start, B)], tile.at[pl.ds(s * B, B)], tile_sem.at[s]))
+        tiles.append(pltpu.make_async_copy(abar.at[pl.ds(start, B)], tile.at[pl.ds(s * B, B)], sem("tile", s)))
     for copy in tiles:
         copy.start()
 
@@ -123,37 +168,31 @@
         k: remote(
             cols_raw.at[0 if k <= ACROSS else 2 * ACROSS],
             cols_raw.at[2 * opposite(k)],
-            cp_recv.at[opposite(k)],
+            sem("plane", opposite(k)),
             at_plane(k if k <= ACROSS else PSLOT[PLANE[k][0], 0]),
         )
         for k in range(1, 8)
     }
-    from_plane = {
-        k: remote(cols_raw.at[0], cols_raw.at[2 * k], cp_recv.at[k], at_plane(1)) for k in range(1, 8)
-    }
     to_core = {
-        k: remote(cols_raw.at[2 * k], cols_raw.at[2 * k + 1], cd_recv.at[k], at_core) for k in range(8)
+        k: remote(cols_raw.at[2 * k], cols_raw.at[2 * k + 1], sem("core", k), at_core) for k in range(8)
     }
     to_z = {
-        d: remote(rows_raw.at[own], rows_raw.at[POS[-d % 8, 0]], rz_recv.at[ZSLOT[-d % 8]], at_z(d))
+        d: remote(rows_raw.at[own], rows_raw.at[POS[-d % 8, 0]], sem("z", -d), at_z(d))
         for d in (1, -1, 2, -2)
     }
     for d in (3, -3):
         step = d // 3
         to_z[d] = remote(
-            rows_raw.at[POS[-2 * step % 8, 0]], rows_raw.at[POS[-d % 8, 0]], rz_recv.at[ZSLOT[-d % 8]], at_z(step)
+            rows_raw.at[POS[-2 * step % 8, 0]], rows_raw.at[POS[-d % 8, 0]], sem("z", -d), at_z(step)
         )
     to_z[4] = remote(
         rows_raw.at[jnp.where(core == 0, POS[-2 % 8, 0], POS[2, 0])],
         rows_raw.at[POS[4, 0]],
-        rz_recv.at[ZSLOT[4]],
+        sem("z", 4),
         at_z(2 - 4 * core),
     )
-    from_z = {
-        d: remote(rows_raw.at[own], rows_raw.at[POS[d % 8, 0]], rz_recv.at[ZSLOT[d % 8]], at_z(1)) for d in ZS[1:]
-    }
     to_y = {
-        d: remote(rows_raw.at[POS[d % 8, 0]], rows_raw.at[POS[d % 8, 1]], ry_recv.at[ZSLOT[d % 8]], at_y) for d in ZS
+        d: remote(rows_raw.at[POS[d % 8, 0]], rows_raw.at[POS[d % 8, 1]], sem("y", d), at_y) for d in ZS
     }
     start(to_core[0])
     for k in (4, 3, 1, 2):
@@ -204,7 +243,7 @@
         places.append(pl.multiple_of((2 * k + (a % 2 - core + 2) % 2) * B, B))
 
     def relayout(s):
-        tiles[s].wait()
+        wait_for("tile", s)
 
         def group(g, carry):
             at = pl.ds(pl.multiple_of(s * B + g * 16, 16), 16)
@@ -216,13 +255,11 @@
         lax.fori_loop(0, B // 16, group, 0, unroll=2)
 
     def arrive_z(d):
-        with jax.named_scope(f"z_{d}"):
-            from_z[d].wait_recv()
+        wait_for("z", d)
         start(to_y[d])
 
     def arrive_plane(k):
-        with jax.named_scope(f"plane_{k}"):
-            from_plane[k].wait_recv()
+        wait_for("plane", k)
         start(to_core[k])
 
     with jax.named_scope("relayout"):
@@ -233,6 +270,8 @@
     arrive_plane(ACROSS)
     for k in (7, 6, 5):
         start(to_plane[k])
+    for k in (1, 2, 3):
+        arrive_plane(k)
     for d in (1, -1):
         arrive_z(d)
     with jax.named_scope("relayout2"):
@@ -240,16 +279,12 @@
             relayout(s)
     for d in (2, -2):
         arrive_z(d)
-    for d in (3, -3, 4):
+    for d in (4, 3, -3):
         start(to_z[d])
-    for k in (1, 2, 3):
-        arrive_plane(k)
     for k in range(1, NEAR):
         prepare_col(2 * k)
     def from_core(chips):
-        with jax.named_scope(f"core_{chips[0]}"):
-            for k in chips:
-                to_core[k].wait_recv()
+        wait_for("core", chips[0])
         for k in chips:
             prepare_col(2 * k + 1)
 
@@ -257,39 +292,37 @@
 
     def f_place(g):
         d, h = g
-        if h and d in (3, -3, 4):
-            return (row, (1 - y_lo) * 8 + (z + d + 8) % 8)
-        return at_z(d) if d else at_y
+        return at_y if d == 0 or h and d in FAR else at_z(d)
+
+    def f_from(g):
+        d, h = g
+        return g if h and d in FAR or d in (0, 4) else (-d, h)
+
+    def f_slot(g):
+        d, h = g
+        return POS[d % 8, 1] if h and d in FAR else POS[-d % 8, h]
 
     f_sends = {
-        g: remote(f_out.at[POS[g[0] % 8, g[1]]], f_in.at[POS[-g[0] % 8, g[1]]], f_recv.at[POS[-g[0] % 8, g[1]]], f_place(g))
+        g: remote(f_out.at[POS[g[0] % 8, g[1]]], f_in.at[f_slot(g)], sem("f", f_from(g)), f_place(g))
         for g in GROUPS
         if g != (0, 0)
     }
-    f_arrive = {
-        g: remote(f_out.at[POS[g[0] % 8, g[1]]], f_in.at[POS[g[0] % 8, g[1]]], f_recv.at[POS[g[0] % 8, g[1]]], at_y)
-        for g in GROUPS
-        if g != (0, 0)
-    }
-    d_sends = {k: remote(d_out.at[k], d_in.at[k], d_recv.at[k], at_core) for k in range(8)}
+    d_sends = {k: remote(d_out.at[k], d_in.at[k], sem("d", k), at_core) for k in range(8)}
     p_sends = {
         k: remote(
             p_out.at[k],
             p_in.at[opposite(k)],
-            p_recv.at[opposite(k)],
+            sem("p", opposite(k)),
             at_plane(k),
         )
         for k in range(1, 8)
     }
-    p_arrive = {k: remote(p_out.at[k], p_in.at[k], p_recv.at[k], at_plane(1)) for k in range(1, 8)}
-
     def first_terms(s):
         both = prods[pl.ds(s * B, B), :]
         return both[:, B:] * left[pl.ds(s * B, B), :B].astype(f32) - both[:, :B]
 
     def arrived(g):
-        with jax.named_scope(f"f_{g[0]}_{g[1]}"):
-            f_arrive[g].wait_recv()
+        wait_for("f", g)
         return f_in[POS[g[0] % 8, g[1]]].astype(f32)
 
     def give_first(g):
@@ -298,6 +331,8 @@
         if g == (0, 1):
             for d in (1, -1, 2, -2):
                 terms += arrived((d, 1))
+        if g[0] in FAR and g[1] == 0:
+            terms += arrived((g[0], 1))
         f_out[s] = terms.astype(bf16)
         pending.append(f_sends[g])
 
@@ -343,8 +378,7 @@
         if g == (0, 0):
             return
         if h == 1:
-            with jax.named_scope(f"y_{d}"):
-                to_y[d].wait_recv()
+            wait_for("y", d)
 
     pending = []
 
@@ -357,8 +391,7 @@
         pending.append(d_sends[k])
 
     def give_plane(k):
-        with jax.named_scope(f"d_{k}"):
-            d_sends[k].wait_recv()
+        wait_for("d", k)
         terms = second_terms(2 * k) + d_in[k].astype(f32)
         p_out[k] = terms.astype(bf16)
         pending.append(p_sends[k])
@@ -379,23 +412,29 @@
         if t == 2:
             arrive_plane(6)
             arrive_plane(5)
-            arrive_z(3)
-            arrive_z(-3)
+        if t == 4:
+            from_core(range(NEAR, 8))
         if t == 3:
-            arrive_plane(7)
             for k in range(NEAR, 8):
                 prepare_col(2 * k)
-        if t == 4:
-            arrive_z(4)
-            from_core(range(NEAR, 8))
-        nexts = fresh(t + 1) if t + 1 < len(UNITS) else ()
-        for g in nexts:
-            need(g)
+        nexts = []
+        for u in (t, t + 1):
+            if u < len(UNITS) and (u == t or u not in LATE):
+                for g in fresh(u):
+                    need(g)
+                    ready.add(g)
+                    if u == t:
+                        prepare_row(POS[g[0] % 8, g[1]])
+                    else:
+                        nexts.append(g)
+        if t == 2:
+            arrive_plane(7)
+            for d in (4, 3, -3):
+                arrive_z(d)
         if t < len(UNITS):
             make_weights(t)
         for g in nexts:
             prepare_row(POS[g[0] % 8, g[1]])
-            ready.add(g)
         if t > 0:
             use_weights(t - 1)
         if t > 0 and UNITS[t - 1][0] == 2 * len(PAIRS):
@@ -403,33 +442,36 @@
                 give_core(k)
                 core_done[k] = t
         for g in GROUPS:
-            if done[g] == t and t < len(UNITS):
+            if done[g] == t and t < len(UNITS) and g not in ((0, 1), (4, 0)):
                 give_first(g)
         while p_queue and core_done.get(p_queue[0], t) + NEXT_P <= t:
             give_plane(p_queue.pop(0))
     flush()
-    for g in ((1, 0), (-1, 0)):
+    while p_queue and p_queue[0] > 3:
+        give_plane(p_queue.pop(0))
+        if len(pending) > 1:
+            start(pending.pop(0))
+    for g in ((4, 0), (3, 0), (-3, 0)):
         give_first(g)
         if len(pending) > 1:
             start(pending.pop(0))
     while p_queue and p_queue[0] > 1:
         give_plane(p_queue.pop(0))
         start(pending.pop(0))
-    give_first((0, 1))
-    start(pending.pop(0))
+    for g in ((-1, 0), (0, 1)):
+        give_first(g)
+        start(pending.pop(0))
     give_plane(1)
     flush()
-    with jax.named_scope("d_0"):
-        d_sends[0].wait_recv()
+    wait_for("d", 0)
     mine_t = second_terms(0) + d_in[0].astype(f32)
     mine = first_terms(own)
     flush()
     for k in reversed(range(1, 8)):
-        with jax.named_scope(f"p_{k}"):
-            p_arrive[k].wait_recv()
+        wait_for("p", k)
         mine_t += p_in[k].astype(f32)
     mine += mine_t.T
-    for g in ((2, 0), (-2, 0), (3, 0), (-3, 0), (4, 0), (3, 1), (-3, 1), (4, 1), (1, 0), (-1, 0), (0, 1)):
+    for g in ((2, 0), (-2, 0), (1, 0), (-1, 0), (0, 1), (3, 0), (-3, 0), (4, 0)):
         mine += arrived(g)
     out[...] = mine
     all_sent = flat.at[pl.ds(0, len(n_sent) * B * B // N)]
@@ -451,8 +493,7 @@
             vmem((N, 2 * B), bf16), vmem((2 * B, N), bf16), vmem((N, 2 * B), bf16), vmem((B + 16, N), bf16),
             vmem((2, 4 * B, N), bf16), vmem((N, 2 * B), f32), vmem((B + 16, N), f32),
             blocks(16), blocks(16), *[blocks(8) for _ in range(4)],
-            dma((3,)), dma((16,)), dma,
-            *[dma((8,)) for _ in range(6)], dma((16,)),
+            dma((len(COPIES),)), dma,
         ],
         compiler_params=pltpu.CompilerParams(
             collective_id=0, has_side_effects=True, vmem_limit_bytes=40 * 2**20

time: 36.1 us -> 33.2 us (0.920); the launches traced: 36 us -> 32.6 us
  Pallas kernels: 35.3 us -> 31.9 us
    pallas_call x1, Pallas kernels: 35.3 us -> 31.9 us  [per_device(): pl.pallas_call(kernel, out_shape=jax.ShapeDtypeStruct((B, B), f32), in_sp...]
where the time goes in v3:
time: 33.2 us; the launch traced here: 32.6 us
  Pallas kernels  31.9 us (96%)
  other arithmetic  0.64 us (2%)
    pallas_call x1, Pallas kernels, per_device(): pl.pallas_call(kernel, out_shape=jax.ShapeDtypeStruct((B, B), f32), in_sp...  31.9 us

profile of v3, /device:TPU:32, one launch (start us, length us, event | category | flops | bytes accessed | tf_op | source)
XLA Modules:
  0.0 32.6 jit_solution(9692508404961422659)
XLA Ops:
  0.0 0.0 copy-start
  0.0 31.9 %shard_map.37 = f32[128,128]{1,0:T(8,128)S(1)} custom-call(bf16[128,128]{1,0:T(8,128)(2,1)} %points.1, bf16[2048,16,128]{2,1,0:T(8,128)(2,1)} %bitcast.2, f32[1,128]{1,0:T(1,128)} %bitcast.3), custom_call_target="tpu_custom_call" | custom-call | tf_op jit(solution)/shard_map/pallas_call | solution.py:485
  31.9 0.0 copy-done
  31.9 0.6 %negate_multiply_fusion = f32[128,128]{1,0:T(8,128)} fusion(f32[128,128]{1,0:T(8,128)S(1)} %shard_map.37, f32[128]{0:T(128)S(1)} %copy-done), kind=kLoop, calls=%fused_computation | loop fusion | flops 32768 | bytes 131584 | tf_op jit(solution)/shard_map/mul | solution.py:502
Async XLA Ops:
  0.0 31.9 %copy-start = (f32[128]{0:T(128)S(1)}, f32[128]{0:T(128)}, u32[]{:S(2)}) copy-start(f32[128]{0:T(128)} %param.5) | copy-start | bytes 1540

commit v4 on v3

--- a/solution.py
+++ b/solution.py
@@ -70,6 +70,7 @@
 )
 COPIES = tuple(tuple(c) for c in SETS)
 LATE = (2, 6, 7)
+EXTRA = {3: (-1, 0), 4: (3, 0), 5: (-3, 0)}
 EARLY = 12
 NEXT_P = 2
 
@@ -274,13 +275,13 @@
         arrive_plane(k)
     for d in (1, -1):
         arrive_z(d)
-    with jax.named_scope("relayout2"):
-        for s in range(EARLY, 16):
-            relayout(s)
     for d in (2, -2):
         arrive_z(d)
     for d in (4, 3, -3):
         start(to_z[d])
+    with jax.named_scope("relayout2"):
+        for s in range(EARLY, 16):
+            relayout(s)
     for k in range(1, NEAR):
         prepare_col(2 * k)
     def from_core(chips):
@@ -357,14 +358,14 @@
         first, n, low, high = UNITS[u]
         rows, cs = pl.ds(first * B, n * B), slice(low * 2 * B, high * 2 * B)
         held = weights[u % 2, : n * B, cs]
-        part = jnp.dot(held, right[cs, :], preferred_element_type=f32)
-        for at, new in ((slice(i * B, (i + 1) * B), first + i) for i in range(n)):
-            to = pl.ds(new * B, B)
-            if new in seen_rows:
-                prods[to, :] += part[at]
+        for i in range(0, n, 2):
+            part = jnp.dot(held[i * B : (i + 2) * B], right[cs, :], preferred_element_type=f32)
+            to = pl.ds((first + i) * B, 2 * B)
+            if first + i in seen_rows:
+                prods[to, :] += part
             else:
-                prods[to, :] = part[at]
-            seen_rows.add(new)
+                prods[to, :] = part
+            seen_rows.add(first + i)
         term = jnp.dot(left_t[:, rows], held, preferred_element_type=f32)
         if low in seen_cols:
             second_t[:, cs] += term
@@ -427,6 +428,9 @@
                         prepare_row(POS[g[0] % 8, g[1]])
                     else:
                         nexts.append(g)
+        if t in EXTRA:
+            nexts.append(EXTRA[t])
+            ready.add(EXTRA[t])
         if t == 2:
             arrive_plane(7)
             for d in (4, 3, -3):
@@ -458,14 +462,14 @@
     while p_queue and p_queue[0] > 1:
         give_plane(p_queue.pop(0))
         start(pending.pop(0))
-    for g in ((-1, 0), (0, 1)):
-        give_first(g)
-        start(pending.pop(0))
+    give_first((-1, 0))
+    start(pending.pop(0))
     give_plane(1)
     flush()
-    wait_for("d", 0)
     mine_t = second_terms(0) + d_in[0].astype(f32)
     mine = first_terms(own)
+    flush()
+    give_first((0, 1))
     flush()
     for k in reversed(range(1, 8)):
         wait_for("p", k)

time: 33.2 us -> 32.6 us (0.982); the launches traced: 32.6 us -> 32.4 us
  no operation moved by 1% of the time
where the time goes in v4:
time: 32.6 us; the launch traced here: 32.4 us
  Pallas kernels  31.7 us (97%)
  other arithmetic  0.64 us (2%)
    pallas_call x1, Pallas kernels, per_device(): pl.pallas_call(kernel, out_shape=jax.ShapeDtypeStruct((B, B), f32), in_sp...  31.7 us

profile of v4, /device:TPU:32, one launch (start us, length us, event | category | flops | bytes accessed | tf_op | source)
XLA Modules:
  0.0 32.4 jit_solution(2736631342856593774)
XLA Ops:
  0.0 0.0 copy-start
  0.0 31.7 %shard_map.37 = f32[128,128]{1,0:T(8,128)S(1)} custom-call(bf16[128,128]{1,0:T(8,128)(2,1)} %points.1, bf16[2048,16,128]{2,1,0:T(8,128)(2,1)} %bitcast.2, f32[1,128]{1,0:T(1,128)} %bitcast.3), custom_call_target="tpu_custom_call" | custom-call | tf_op jit(solution)/shard_map/pallas_call | solution.py:489
  31.8 0.0 copy-done
  31.8 0.6 %negate_multiply_fusion = f32[128,128]{1,0:T(8,128)} fusion(f32[128,128]{1,0:T(8,128)S(1)} %shard_map.37, f32[128]{0:T(128)S(1)} %copy-done), kind=kLoop, calls=%fused_computation | loop fusion | flops 32768 | bytes 131584 | tf_op jit(solution)/shard_map/mul | solution.py:506
Async XLA Ops:
  0.0 31.8 %copy-start = (f32[128]{0:T(128)S(1)}, f32[128]{0:T(128)}, u32[]{:S(2)}) copy-start(f32[128]{0:T(128)} %param.5) | copy-start | bytes 1540

commit v5 on v4

--- a/solution.py
+++ b/solution.py
@@ -413,6 +413,7 @@
         if t == 2:
             arrive_plane(6)
             arrive_plane(5)
+            arrive_plane(7)
         if t == 4:
             from_core(range(NEAR, 8))
         if t == 3:
@@ -432,7 +433,6 @@
             nexts.append(EXTRA[t])
             ready.add(EXTRA[t])
         if t == 2:
-            arrive_plane(7)
             for d in (4, 3, -3):
                 arrive_z(d)
         if t < len(UNITS):

time: 32.6 us -> 32.4 us (level)
  no operation moved by 1% of the time
where the time goes in v5:
time: 32.4 us; the launch traced here: 32.2 us
  Pallas kernels  31.6 us (98%)
  other arithmetic  0.64 us (2%)
    pallas_call x1, Pallas kernels, per_device(): pl.pallas_call(kernel, out_shape=jax.ShapeDtypeStruct((B, B), f32), in_sp...  31.6 us

profile of v5, /device:TPU:32, one launch (start us, length us, event | category | flops | bytes accessed | tf_op | source)
XLA Modules:
  0.0 32.2 jit_solution(10148781023316156470)
XLA Ops:
  0.0 0.0 copy-start
  0.0 31.6 %shard_map.37 = f32[128,128]{1,0:T(8,128)S(1)} custom-call(bf16[128,128]{1,0:T(8,128)(2,1)} %points.1, bf16[2048,16,128]{2,1,0:T(8,128)(2,1)} %bitcast.2, f32[1,128]{1,0:T(1,128)} %bitcast.3), custom_call_target="tpu_custom_call" | custom-call | tf_op jit(solution)/shard_map/pallas_call | solution.py:489
  31.6 0.0 copy-done
  31.6 0.6 %negate_multiply_fusion = f32[128,128]{1,0:T(8,128)} fusion(f32[128,128]{1,0:T(8,128)S(1)} %shard_map.37, f32[128]{0:T(128)S(1)} %copy-done), kind=kLoop, calls=%fused_computation | loop fusion | flops 32768 | bytes 131584 | tf_op jit(solution)/shard_map/mul | solution.py:506
Async XLA Ops:
  0.0 31.6 %copy-start = (f32[128]{0:T(128)S(1)}, f32[128]{0:T(128)}, u32[]{:S(2)}) copy-start(f32[128]{0:T(128)} %param.5) | copy-start | bytes 1540
